TPU v7x, 32 devices: a whole 2x2x4 slice. The times are simulated.
32 devices in a mesh: grp: 16 (over z, y, x), sub: 2 (over core).
Axes of the slice: x: 2, y: 2, z: 4, core: 2. Of those that a mesh axis runs over, the one named last changes fastest.
Arguments:
- potentials: bfloat16 [1024, 200, 200], P(('grp', 'sub')), may hold values from -6 to 6
- dimers: int32 [4096, 2], P(('grp', 'sub')), may hold values from 0 to 1023, as said below
- coupling: float32 [4096], P(('grp', 'sub')), may hold values from 0.3 to 1.5
- transform: bfloat16 [400, 400], replicated, may hold values from -0.3125 to 0.3125
Outputs:
- energies: float32 [4096, 400], P(('grp', 'sub'))
- checksum: float32 [1], replicated
Inputs may be any that keep to these rules, and one draw needn't show every extreme that they name: `dimers`: each row names two different fragments. Rows d with d // 128 = o belong to owner o, and their second fragment f has f // 32 = o. Among the 128 first fragments of one owner's rows, at most 6 fall into the fragments of any one device (fragments f with f // 32 equal), and exactly 6 into some device's fragments.
All inputs are finite; a program needn't handle non-finite values.
Results may differ from a plain program's by a relative error of at most 0.0023.
Values may be sent and summed in bfloat16 or wider, within the bound.
No kernel may reach another device: no remote copies, remote signals or barrier semaphores. Data moves between devices by JAX's collectives and lax.ppermute only.
A program may use at most 192 MiB of HBM per device.

v0:
```python
import jax
import jax.numpy as jnp
from jax import lax
from jax.sharding import PartitionSpec as P


def block_energies(left, right, scale, transform, basis):
    upper = transform[:basis]
    lower = transform[basis:]
    cross = jnp.einsum("nab,nbc->nac", left, right, preferred_element_type=jnp.float32)
    block = (cross * (scale[:, None, None] / jnp.sqrt(jnp.float32(basis)))).astype(jnp.bfloat16)
    top = jnp.einsum("nab,bk->nak", left, upper, preferred_element_type=jnp.float32)
    top = top + jnp.einsum("nab,bk->nak", block, lower, preferred_element_type=jnp.float32)
    bottom = jnp.einsum("nab,ak->nbk", block, upper, preferred_element_type=jnp.float32)
    bottom = bottom + jnp.einsum("nab,bk->nak", right, lower, preferred_element_type=jnp.float32)
    upper_f = upper.astype(jnp.float32)
    lower_f = lower.astype(jnp.float32)
    return jnp.sum(upper_f[None] * top, axis=1) + jnp.sum(lower_f[None] * bottom, axis=1)


def local(potentials, dimers, coupling, transform):
    frag_dev, basis, _ = potentials.shape
    count = dimers.shape[0]
    owners = lax.axis_size(("grp", "sub"))
    cap = max(2, (4 * count + 3 * owners - 1) // (3 * owners))
    wanted = dimers[:, 0]
    source = wanted // frag_dev
    onehot = (source[:, None] == jnp.arange(owners, dtype=jnp.int32)[None, :]).astype(jnp.int32)
    ranking = jnp.sum(jnp.cumsum(onehot, axis=0) * onehot, axis=1) - 1
    slots = source * cap + ranking
    requests = jnp.zeros((owners * cap,), jnp.int32).at[slots].set(wanted % frag_dev)
    asked = lax.all_to_all(
        requests.reshape(owners, cap), ("grp", "sub"), split_axis=0, concat_axis=0, tiled=True
    )
    served = jnp.take(potentials, asked.reshape(-1), axis=0).reshape(owners, cap, basis, basis)
    arrived = lax.all_to_all(served, ("grp", "sub"), split_axis=0, concat_axis=0, tiled=True)
    leading = jnp.take(arrived.reshape(owners * cap, basis, basis), slots, axis=0)
    trailing = jnp.take(potentials, dimers[:, 1] % frag_dev, axis=0)
    width = 8
    leading = leading.reshape(count // width, width, basis, basis)
    trailing = trailing.reshape(count // width, width, basis, basis)
    scales = coupling.reshape(count // width, width)

    def one_block(item):
        left, right, scale = item
        return block_energies(left, right, scale, transform, basis)

    energies = lax.map(one_block, (leading, trailing, scales)).reshape(count, 2 * basis)
    total = count * owners
    position = lax.axis_index(("grp", "sub")) * count + jnp.arange(count, dtype=jnp.int32)
    weights = (position.astype(jnp.float32) + 1.0) / total
    partial_value = 2.0 / total * jnp.sum(weights * jnp.mean(energies * energies, axis=1))
    checksum = lax.psum(partial_value, ("grp", "sub"))
    return (energies, checksum.reshape(1))


def solution(mesh):
    in_specs = (P(("grp", "sub"), None, None), P(("grp", "sub"), None), P(("grp", "sub")), P())
    out_specs = (P(("grp", "sub"), None), P())
    return jax.shard_map(local, mesh=mesh, in_specs=in_specs, out_specs=out_specs, check_vma=False)
```

profile of v0, /device:TPU:12, one launch (start us, length us, event | category | flops | bytes accessed | tf_op | source)
XLA Modules:
  0.0 666.5 jit_solution(18246285668778304363)
XLA Ops:
  0.6 0.8 fusion.30
  1.5 0.8 and_select_fusion.1
  2.8 1.3 and_reduce_fusion
  4.0 1.0 scatter_custom_fusion
  5.1 10.9 %all_to_all.14 = s32[32,1,6]{2,1,0:T(1,128)S(1)} all-to-all(s32[32,1,6]{2,1,0:T(1,128)S(1)} %bitcast.75), channel_id=1, replica_groups=mesh['grp'=16,'sub'=2] {'grp','sub'}, dimensions={0} | all-to-all | bytes 1536 | tf_op jit(solution)/shard_map/all_to_all | solution.py:32
  17.5 10.6 %gather_fusion = bf16[192,200,200]{2,1,0:T(8,128)(2,1)} fusion(bf16[32,200,200]{2,1,0:T(8,128)(2,1)S(1)} %copy-done, s32[1024]{0:T(1024)S(1)} %pad_clamp_fusion.2), kind=kCustom, calls=%fused_computation | custom fusion | bytes 30720768 | tf_op jit(solution)/shard_map/jit(_take)/gather | solution.py:35
  28.1 17.0 %broadcast_select_fusion = bf16[32,6,200,200]{3,2,1,0:T(8,128)(2,1)} fusion(bf16[32,6,200,200]{3,2,1,0:T(8,128)(2,1)} %bitcast.70, pred[32,6]{1,0:T(8,128)(4,1)S(1)} %compare_and_fusion), kind=kLoop, calls=%fused_computation.34 | loop fusion | flops 7680000 | bytes 30720192 | tf_op jit(solution)/shard_map/jit(_take)/select_n | solution.py:35
  45.1 5.9 all-to-all-start.1
  51.8 8.7 %gather_fusion.2 = bf16[128,200,200]{2,1,0:T(8,128)(2,1)} fusion(bf16[32,200,200]{2,1,0:T(8,128)(2,1)S(1)} %copy-done, s32[1024]{0:T(1024)S(1)} %pad_clamp_fusion), kind=kCustom, calls=%fused_computation.2 | custom fusion | bytes 20480512 | tf_op jit(solution)/shard_map/jit(_take)/gather | solution.py:38
  61.3 10.1 %broadcast_select_fusion.1 = bf16[16,8,200,200]{3,2,1,0:T(8,128)(2,1)} fusion(bf16[16,8,200,200]{3,2,1,0:T(8,128)(2,1)} %bitcast.71, pred[16,8]{1,0:T(8,128)(4,1)S(1)} %broadcast_in_dim.59), kind=kLoop, calls=%fused_computation.35 | loop fusion | flops 5120000 | bytes 20480128 | tf_op jit(solution)/shard_map/jit(_take)/select_n | solution.py:38
  71.5 401.6 %all-to-all-done.1 = bf16[32,6,200,200]{3,2,1,0:T(8,128)(2,1)} async-done(((bf16[32,6,200,200]{3,2,1,0:T(8,128)(2,1)}), bf16[32,6,200,200]{3,2,1,0:T(8,128)(2,1)}, u32[]{:S(2)}, u32[]{:S(2)}) %all-to-all-start.1) | async-done | bytes 15360032 | tf_op jit(solution)/shard_map/all_to_all | solution.py:36
  473.1 15.3 %gather_fusion.1 = bf16[128,200,200]{2,1,0:T(8,128)(2,1)} fusion(bf16[192,200,200]{2,1,0:T(8,128)(2,1)} %bitcast.14, s32[1024]{0:T(1024)S(1)} %pad_clamp_fusion.1), kind=kCustom, calls=%fused_computation.1 | custom fusion | bytes 20480512 | tf_op jit(solution)/shard_map/jit(_take)/gather | solution.py:37
  488.3 10.2 %broadcast_select_fusion.2 = bf16[16,8,200,200]{3,2,1,0:T(8,128)(2,1)} fusion(bf16[16,8,200,200]{3,2,1,0:T(8,128)(2,1)} %bitcast.72, pred[16,8]{1,0:T(8,128)(4,1)S(1)} %broadcast_in_dim.51), kind=kLoop, calls=%fused_computation.36 | loop fusion | flops 5120000 | bytes 20480128 | tf_op jit(solution)/shard_map/jit(_take)/select_n | solution.py:37
  498.6 110.3 %while.10 = (s32[]{:T(128)}, f32[16,8,400]{2,1,0:T(8,128)S(1)}, bf16[400,400]{1,0:T(8,128)(2,1)S(1)}, bf16[16,8,200,200]{3,2,1,0:T(8,128)(2,1)}, bf16[16,8,200,2...) while((s32[]{:T(128)}, f32[16,8,400]{2,1,0:T(8,128)S(1)}, bf16[400,400]{1,0:T(8,128)(2,1)S(1)}, ...), condition=%wide.region_6.7_spmd, body=%wide.region_3.6_spmd.sunk | while | flops 1156636800 | bytes 19904180 | solution.py:48
  498.6 1.8 multiply_convert_fusion.2
  500.3 1.7 fusion.54
  503.6 1.9 multiply_reduce_fusion.7
  505.5 1.8 multiply_convert_fusion.2
  507.2 1.7 fusion.54
  510.5 1.9 multiply_reduce_fusion.7
  512.4 1.8 multiply_convert_fusion.2
  514.1 1.7 fusion.54
  517.3 1.9 multiply_reduce_fusion.7
  519.3 1.8 multiply_convert_fusion.2
  521.0 1.7 fusion.54
  524.2 1.9 multiply_reduce_fusion.7
  526.2 1.8 multiply_convert_fusion.2
  527.9 1.7 fusion.54
  531.1 1.9 multiply_reduce_fusion.7
  533.1 1.8 multiply_convert_fusion.2
  534.8 1.7 fusion.54
  538.0 1.9 multiply_reduce_fusion.7
  539.9 1.8 multiply_convert_fusion.2
  541.7 1.7 fusion.54
  544.9 1.9 multiply_reduce_fusion.7
  546.8 1.8 multiply_convert_fusion.2
  548.6 1.7 fusion.54
  551.8 1.9 multiply_reduce_fusion.7
  553.7 1.8 multiply_convert_fusion.2
  555.5 1.7 fusion.54
  558.7 1.9 multiply_reduce_fusion.7
  560.6 1.8 multiply_convert_fusion.2
  562.4 1.7 fusion.54
  565.6 1.9 multiply_reduce_fusion.7
  567.5 1.8 multiply_convert_fusion.2
  569.3 1.7 fusion.54
  572.5 1.9 multiply_reduce_fusion.7
  574.4 1.8 multiply_convert_fusion.2
  576.2 1.7 fusion.54
  579.4 1.9 multiply_reduce_fusion.7
  581.3 1.8 multiply_convert_fusion.2
  583.1 1.7 fusion.54
  586.3 1.9 multiply_reduce_fusion.7
  588.2 1.8 multiply_convert_fusion.2
  590.0 1.7 fusion.54
  593.2 1.9 multiply_reduce_fusion.7
  595.1 1.8 multiply_convert_fusion.2
  596.9 1.7 fusion.54
  600.1 1.9 multiply_reduce_fusion.7
  602.0 1.8 multiply_convert_fusion.2
  603.8 1.7 fusion.54
  607.0 1.9 multiply_reduce_fusion.7
  610.5 55.1 %psum.7 = f32[1]{0:T(128)} all-reduce(f32[1]{0:T(128)} %bitcast.19), channel_id=1, replica_groups=mesh['grp'=16,'sub'=2] {'grp','sub'}, use_global_device_ids=true, to_apply=%region_9.10 | all-reduce | flops 1 | bytes 8 | tf_op jit(solution)/shard_map/psum | solution.py:53
  665.6 0.8 copy.23
  (105 shorter events, 28.0 us)
Async XLA Ops:
  0.6 16.8 %copy-start = (bf16[32,200,200]{2,1,0:T(8,128)(2,1)S(1)}, bf16[32,200,200]{2,1,0:T(8,128)(2,1)}, u32[]{:S(2)}) copy-start(bf16[32,200,200]{2,1,0:T(8,128)(2,1)} %param.6) | copy-start | bytes 7680004
  45.1 427.9 %all-to-all-start.1 = ((bf16[32,6,200,200]{3,2,1,0:T(8,128)(2,1)}), bf16[32,6,200,200]{3,2,1,0:T(8,128)(2,1)}, u32[]{:S(2)}, u32[]{:S(2)}) async-start(bf16[32,6,200,200]{3,2,1,0:T(8,128)(2,1)} %broadcast_select_fusion), calls=%async_computation.1 | async-start | bytes 39321600 | tf_op jit(solution)/shard_map/all_to_all | solution.py:36
  488.3 10.2 %copy-start.2 = (bf16[400,400]{1,0:T(8,128)(2,1)S(1)}, bf16[400,400]{1,0:T(8,128)(2,1)}, u32[]{:S(2)}) copy-start(bf16[400,400]{1,0:T(8,128)(2,1)} %param.9) | copy-start | bytes 960004
  608.9 57.6 %copy-start.1 = (bf16[32,200,200]{2,1,0:T(8,128)(2,1)S(1)}, bf16[32,200,200]{2,1,0:T(8,128)(2,1)}, u32[]{:S(2)}) copy-start(bf16[32,200,200]{2,1,0:T(8,128)(2,1)} %param.6) | copy-start | bytes 7680004
where the time goes:
time: 669 us; the launch traced here: 666 us
  waiting for transfers between devices  402 us (60%)
  matrix products  108 us (16%)
  blocking collectives  66 us (10%)
  other arithmetic  44.6 us (7%)
  local copies, waits for them, and re-layouts  38.2 us (6%)
    all_to_all x1, waiting for transfers between devices, local(): lax.all_to_all(served, ('grp', 'sub'), split_axis=0, concat_axis=0, tiled...  402 us
    psum x1, blocking collectives, local(): checksum = lax.psum(partial_value, ('grp', 'sub'))  55.1 us
    dot_general x16, matrix products, block_energies(): jnp.einsum('nab,bk->nak', right, lower, preferred_element_type=jnp.float32)  29.7 us
    dot_general x16, matrix products, block_energies(): jnp.einsum('nab,nbc->nac', left, right, preferred_element_type=jnp.float32)  28.3 us
    dot_general x16, matrix products, block_energies(): jnp.einsum('nab,bk->nak', left, upper, preferred_element_type=jnp.float32)  27.7 us
    select_n x2, other arithmetic, local(): jnp.take(potentials, asked.reshape(-1), axis=0)  17 us
    gather x1, local copies, waits for them, and re-layouts, local(): jnp.take(arrived.reshape(owners * cap, basis, basis), slots, axis=0)  15.3 us
  transfers between devices with their start and end apart: 1, of which 1 were waited for; matrix products, arithmetic and copies ran while one was open for 3% of the time, Pallas kernels for 0%

commit v1 on v0

--- a/solution.py
+++ b/solution.py
@@ -50,7 +50,7 @@
     position = lax.axis_index(("grp", "sub")) * count + jnp.arange(count, dtype=jnp.int32)
     weights = (position.astype(jnp.float32) + 1.0) / total
     partial_value = 2.0 / total * jnp.sum(weights * jnp.mean(energies * energies, axis=1))
-    checksum = lax.psum(partial_value, ("grp", "sub"))
+    checksum = jnp.sum(lax.all_gather(partial_value, ("grp", "sub")), axis=0)
     return (energies, checksum.reshape(1))
 
 

time: 669 us -> 669 us (level)
    psum x1 -> x0, blocking collectives: 55.1 us -> none  [local(): checksum = lax.psum(partial_value, ('grp', 'sub'))]
    unnamed x0 -> x1, blocking collectives: none -> 54.2 us
where the time goes in v1:
time: 669 us; the launch traced here: 666 us
  waiting for transfers between devices  402 us (60%)
  matrix products  108 us (16%)
  blocking collectives  65 us (10%)
  other arithmetic  45.2 us (7%)
  local copies, waits for them, and re-layouts  38.3 us (6%)
    all_to_all x1, waiting for transfers between devices, local(): lax.all_to_all(served, ('grp', 'sub'), split_axis=0, concat_axis=0, tiled...  402 us
    unnamed x1, blocking collectives  54.2 us
    dot_general x16, matrix products, block_energies(): jnp.einsum('nab,bk->nak', right, lower, preferred_element_type=jnp.float32)  29.7 us
    dot_general x16, matrix products, block_energies(): jnp.einsum('nab,nbc->nac', left, right, preferred_element_type=jnp.float32)  28.3 us
    dot_general x16, matrix products, block_energies(): jnp.einsum('nab,bk->nak', left, upper, preferred_element_type=jnp.float32)  27.7 us
    select_n x2, other arithmetic, local(): jnp.take(potentials, asked.reshape(-1), axis=0)  17 us
    gather x1, local copies, waits for them, and re-layouts, local(): jnp.take(arrived.reshape(owners * cap, basis, basis), slots, axis=0)  15.3 us
  transfers between devices with their start and end apart: 1, of which 1 were waited for; matrix products, arithmetic and copies ran while one was open for 3% of the time, Pallas kernels for 0%

profile of v1, /device:TPU:12, one launch (start us, length us, event | category | flops | bytes accessed | tf_op | source)
XLA Modules:
  0.0 666.2 jit_solution(16908118821796944188)
XLA Ops:
  0.6 0.8 fusion.30
  1.5 0.8 and_select_fusion.1
  2.8 1.3 and_reduce_fusion
  4.0 1.0 scatter_custom_fusion
  5.1 10.9 %all_to_all.14 = s32[32,1,6]{2,1,0:T(1,128)S(1)} all-to-all(s32[32,1,6]{2,1,0:T(1,128)S(1)} %bitcast.76), channel_id=1, replica_groups=mesh['grp'=16,'sub'=2] {'grp','sub'}, dimensions={0} | all-to-all | bytes 1536 | tf_op jit(solution)/shard_map/all_to_all | solution.py:32
  17.5 10.6 %gather_fusion = bf16[192,200,200]{2,1,0:T(8,128)(2,1)} fusion(bf16[32,200,200]{2,1,0:T(8,128)(2,1)S(1)} %copy-done, s32[1024]{0:T(1024)S(1)} %pad_clamp_fusion.2), kind=kCustom, calls=%fused_computation | custom fusion | bytes 30720768 | tf_op jit(solution)/shard_map/jit(_take)/gather | solution.py:35
  28.1 17.0 %broadcast_select_fusion = bf16[32,6,200,200]{3,2,1,0:T(8,128)(2,1)} fusion(bf16[32,6,200,200]{3,2,1,0:T(8,128)(2,1)} %bitcast.71, pred[32,6]{1,0:T(8,128)(4,1)S(1)} %compare_and_fusion), kind=kLoop, calls=%fused_computation.34 | loop fusion | flops 7680000 | bytes 30720192 | tf_op jit(solution)/shard_map/jit(_take)/select_n | solution.py:35
  45.1 5.9 all-to-all-start.1
  51.8 8.7 %gather_fusion.2 = bf16[128,200,200]{2,1,0:T(8,128)(2,1)} fusion(bf16[32,200,200]{2,1,0:T(8,128)(2,1)S(1)} %copy-done, s32[1024]{0:T(1024)S(1)} %pad_clamp_fusion), kind=kCustom, calls=%fused_computation.2 | custom fusion | bytes 20480512 | tf_op jit(solution)/shard_map/jit(_take)/gather | solution.py:38
  61.3 10.1 %broadcast_select_fusion.1 = bf16[16,8,200,200]{3,2,1,0:T(8,128)(2,1)} fusion(bf16[16,8,200,200]{3,2,1,0:T(8,128)(2,1)} %bitcast.72, pred[16,8]{1,0:T(8,128)(4,1)S(1)} %broadcast_in_dim.59), kind=kLoop, calls=%fused_computation.35 | loop fusion | flops 5120000 | bytes 20480128 | tf_op jit(solution)/shard_map/jit(_take)/select_n | solution.py:38
  71.5 401.6 %all-to-all-done.1 = bf16[32,6,200,200]{3,2,1,0:T(8,128)(2,1)} async-done(((bf16[32,6,200,200]{3,2,1,0:T(8,128)(2,1)}), bf16[32,6,200,200]{3,2,1,0:T(8,128)(2,1)}, u32[]{:S(2)}, u32[]{:S(2)}) %all-to-all-start.1) | async-done | bytes 15360032 | tf_op jit(solution)/shard_map/all_to_all | solution.py:36
  473.1 15.3 %gather_fusion.1 = bf16[128,200,200]{2,1,0:T(8,128)(2,1)} fusion(bf16[192,200,200]{2,1,0:T(8,128)(2,1)} %bitcast.14, s32[1024]{0:T(1024)S(1)} %pad_clamp_fusion.1), kind=kCustom, calls=%fused_computation.1 | custom fusion | bytes 20480512 | tf_op jit(solution)/shard_map/jit(_take)/gather | solution.py:37
  488.3 10.2 %broadcast_select_fusion.2 = bf16[16,8,200,200]{3,2,1,0:T(8,128)(2,1)} fusion(bf16[16,8,200,200]{3,2,1,0:T(8,128)(2,1)} %bitcast.73, pred[16,8]{1,0:T(8,128)(4,1)S(1)} %broadcast_in_dim.51), kind=kLoop, calls=%fused_computation.36 | loop fusion | flops 5120000 | bytes 20480128 | tf_op jit(solution)/shard_map/jit(_take)/select_n | solution.py:37
  498.6 110.3 %while.10 = (s32[]{:T(128)}, f32[16,8,400]{2,1,0:T(8,128)S(1)}, bf16[400,400]{1,0:T(8,128)(2,1)S(1)}, bf16[16,8,200,200]{3,2,1,0:T(8,128)(2,1)}, bf16[16,8,200,2...) while((s32[]{:T(128)}, f32[16,8,400]{2,1,0:T(8,128)S(1)}, bf16[400,400]{1,0:T(8,128)(2,1)S(1)}, ...), condition=%wide.region_6.7_spmd, body=%wide.region_3.6_spmd.sunk | while | flops 1156636800 | bytes 19904180 | solution.py:48
  498.6 1.8 multiply_convert_fusion.2
  500.3 1.7 fusion.54
  503.6 1.9 multiply_reduce_fusion.7
  505.5 1.8 multiply_convert_fusion.2
  507.2 1.7 fusion.54
  510.5 1.9 multiply_reduce_fusion.7
  512.4 1.8 multiply_convert_fusion.2
  514.1 1.7 fusion.54
  517.3 1.9 multiply_reduce_fusion.7
  519.3 1.8 multiply_convert_fusion.2
  521.0 1.7 fusion.54
  524.2 1.9 multiply_reduce_fusion.7
  526.2 1.8 multiply_convert_fusion.2
  527.9 1.7 fusion.54
  531.1 1.9 multiply_reduce_fusion.7
  533.1 1.8 multiply_convert_fusion.2
  534.8 1.7 fusion.54
  538.0 1.9 multiply_reduce_fusion.7
  539.9 1.8 multiply_convert_fusion.2
  541.7 1.7 fusion.54
  544.9 1.9 multiply_reduce_fusion.7
  546.8 1.8 multiply_convert_fusion.2
  548.6 1.7 fusion.54
  551.8 1.9 multiply_reduce_fusion.7
  553.7 1.8 multiply_convert_fusion.2
  555.5 1.7 fusion.54
  558.7 1.9 multiply_reduce_fusion.7
  560.6 1.8 multiply_convert_fusion.2
  562.4 1.7 fusion.54
  565.6 1.9 multiply_reduce_fusion.7
  567.5 1.8 multiply_convert_fusion.2
  569.3 1.7 fusion.54
  572.5 1.9 multiply_reduce_fusion.7
  574.4 1.8 multiply_convert_fusion.2
  576.2 1.7 fusion.54
  579.4 1.9 multiply_reduce_fusion.7
  581.3 1.8 multiply_convert_fusion.2
  583.1 1.7 fusion.54
  586.3 1.9 multiply_reduce_fusion.7
  588.2 1.8 multiply_convert_fusion.2
  590.0 1.7 fusion.54
  593.2 1.9 multiply_reduce_fusion.7
  595.1 1.8 multiply_convert_fusion.2
  596.9 1.7 fusion.54
  600.1 1.9 multiply_reduce_fusion.7
  602.0 1.8 multiply_convert_fusion.2
  603.8 1.7 fusion.54
  607.0 1.9 multiply_reduce_fusion.7
  610.7 54.2 %all-reduce = f32[32]{0:T(128)S(1)} all-reduce(f32[32]{0:T(128)S(1)} %dynamic-update-slice), channel_id=1, replica_groups=mesh['grp'=16,'sub'=2] {'grp','sub'}, use_global_device_ids=true, to_apply=%add | all-reduce | flops 32 | bytes 256
  665.4 0.8 copy.23
  (108 shorter events, 28.7 us)
Async XLA Ops:
  0.6 16.8 %copy-start = (bf16[32,200,200]{2,1,0:T(8,128)(2,1)S(1)}, bf16[32,200,200]{2,1,0:T(8,128)(2,1)}, u32[]{:S(2)}) copy-start(bf16[32,200,200]{2,1,0:T(8,128)(2,1)} %param.6) | copy-start | bytes 7680004
  45.1 427.9 %all-to-all-start.1 = ((bf16[32,6,200,200]{3,2,1,0:T(8,128)(2,1)}), bf16[32,6,200,200]{3,2,1,0:T(8,128)(2,1)}, u32[]{:S(2)}, u32[]{:S(2)}) async-start(bf16[32,6,200,200]{3,2,1,0:T(8,128)(2,1)} %broadcast_select_fusion), calls=%async_computation.1 | async-start | bytes 39321600 | tf_op jit(solution)/shard_map/all_to_all | solution.py:36
  488.3 10.2 %copy-start.2 = (bf16[400,400]{1,0:T(8,128)(2,1)S(1)}, bf16[400,400]{1,0:T(8,128)(2,1)}, u32[]{:S(2)}) copy-start(bf16[400,400]{1,0:T(8,128)(2,1)} %param.9) | copy-start | bytes 960004
  608.9 57.4 %copy-start.1 = (bf16[32,200,200]{2,1,0:T(8,128)(2,1)S(1)}, bf16[32,200,200]{2,1,0:T(8,128)(2,1)}, u32[]{:S(2)}) copy-start(bf16[32,200,200]{2,1,0:T(8,128)(2,1)} %param.6) | copy-start | bytes 7680004
